TPU v7x, 16 devices: a 4x2x1 block of a 4x4x8 slice. The times are simulated.
16 devices in a mesh: dp: 2 (over y, z), ep: 8 (over x, core).
Axes of the slice: x: 4, y: 2, z: 1, core: 2. Of those that a mesh axis runs over, the one named last changes fastest.
The devices are a block of a 4x4x8 slice.
Arguments:
- hidden: bfloat16 [1024, 2048], P(('dp', 'ep')), parts along dimension 0
- positions: int32 [1024], P(('dp', 'ep')), parts along dimension 0
- expert_ids: int32 [2, 1024, 8], P(None, ('dp', 'ep')), parts along dimension 1
- k_cache: bfloat16 [2, 1024, 16, 16, 128], P(None, ('dp', 'ep')), parts along dimension 1
- v_cache: bfloat16 [2, 1024, 16, 16, 128], P(None, ('dp', 'ep')), parts along dimension 1
- w_query: bfloat16 [2, 2048, 2048], replicated
- w_key: bfloat16 [2, 2048, 2048], replicated
- w_value: bfloat16 [2, 2048, 2048], replicated
- w_out: bfloat16 [2, 2048, 2048], replicated
- attn_gain: float32 [2, 2048], replicated
- q_gain: float32 [2, 2048], replicated
- k_gain: float32 [2, 2048], replicated
- mlp_gain: float32 [2, 2048], replicated
- w_router: bfloat16 [2048, 64], replicated
- w_gate: bfloat16 [64, 2048, 1024], P('ep')
- w_up: bfloat16 [64, 2048, 1024], P('ep')
- w_down: bfloat16 [64, 1024, 2048], P('ep')
Outputs:
- output 1: bfloat16 [1024, 2048], P(('dp', 'ep')), parts along dimension 0
- output 2: bfloat16 [2, 1024, 16, 16, 128], P(None, ('dp', 'ep')), parts along dimension 1
- output 3: bfloat16 [2, 1024, 16, 16, 128], P(None, ('dp', 'ep')), parts along dimension 1
There are 2 independent parts. A program takes and returns all parts, laid end to end along the dimension named above; an argument that names none is the same for every part.
All inputs are finite; a program needn't handle non-finite values.
Results may differ from a plain program's by a relative error of at most 0.02.
Values are sent between devices in bfloat16 or wider.
A program may use at most 768 MiB of HBM per device.

v0:
```python
import functools

import jax
import jax.numpy as jnp
from jax import lax
from jax.experimental import pallas as pl
from jax.experimental.pallas import tpu as pltpu
from jax.sharding import PartitionSpec as P

RMS_EPS = 1e-5
ROPE_BASE = 10000.0
CAP_FACTOR = 2
MESH = pl.DeviceIdType.MESH
AG_PARTS = 2
RS_CHUNKS = 4
UNIT = 1024
RING = 20
COLS = 512
CACHE_BLOCKS = 4
ATTEND_UNROLL = 4


def rms_norm(values, gain_vec):
    values = values.astype(jnp.float32)
    inv_rms = lax.rsqrt(jnp.mean(values * values, axis=-1, keepdims=True) + RMS_EPS)
    return values * inv_rms * gain_vec.astype(jnp.float32)


def rope_tables(positions, head_dim):
    half_dim = head_dim // 2
    frequencies = ROPE_BASE ** (-jnp.arange(half_dim, dtype=jnp.float32) / half_dim)
    angles = positions.astype(jnp.float32)[:, None] * frequencies[None, :]
    cosines, sines = jnp.cos(angles), jnp.sin(angles)
    return jnp.concatenate([cosines, cosines], axis=1), jnp.concatenate([-sines, sines], axis=1)


def attention_kernel(layer, aliased, pos_ref, x_ref, cos_ref, sin_ref, attn_gain, q_gain, k_gain, wq, wk, wv, wo, k_in, v_in, *rest):
    rest = rest[2:] if aliased else rest
    x_out, k_out, v_out, wbuf, kbuf, vbuf, proj, q_rows, k_rows, v_rows, mixed_rows, mixed, w_sem, in_sem, out_sem = rest
    seqs, model = x_ref.shape
    cache_len, heads, head_dim = kbuf.shape[1:]
    cols = wbuf.shape[2]
    chunks = model // cols
    block = seqs // CACHE_BLOCKS

    def weight_copy(index):
        weights = (wq, wk, wv, wo)[index // chunks]
        return pltpu.make_async_copy(weights.at[layer, :, pl.ds((index % chunks) * cols, cols)], wbuf.at[index], w_sem.at[index])

    def cache_in(kind, i):
        source, target = ((k_in, kbuf), (v_in, vbuf))[kind]
        part = pl.ds(i * block, block)
        return pltpu.make_async_copy(source.at[layer, part], target.at[part], in_sem.at[kind, i])

    def cache_out(kind, i):
        source, target = ((kbuf, k_out), (vbuf, v_out))[kind]
        part = pl.ds(i * block, block)
        return pltpu.make_async_copy(source.at[part], target.at[layer, part], out_sem.at[kind, i])

    for index in range(3 * chunks):
        weight_copy(index).start()
    for i in range(CACHE_BLOCKS):
        for kind in range(2):
            cache_in(kind, i).start()
    for index in range(3 * chunks, 4 * chunks):
        weight_copy(index).start()

    normed = rms_norm(x_ref[...], attn_gain[layer:layer + 1, :]).astype(jnp.bfloat16)

    def project(kind):
        for c in range(chunks):
            weight_copy(kind * chunks + c).wait()
            proj[kind, :, c * cols:(c + 1) * cols] = jnp.dot(normed, wbuf[kind * chunks + c], preferred_element_type=jnp.float32)

    def rotate(kind, gain, target):
        values = proj[kind]
        inv_rms = lax.rsqrt(jnp.mean(values * values, axis=-1, keepdims=True) + RMS_EPS)
        cosines, sines = cos_ref[...], sin_ref[...]
        for h in range(heads):
            at = slice(h * head_dim, (h + 1) * head_dim)
            head = proj[kind, :, at] * inv_rms * gain[layer:layer + 1, at]
            turned = head * cosines + pltpu.roll(head, head_dim // 2, 1) * sines
            target[pl.ds(h, seqs, stride=heads), :] = turned.astype(jnp.bfloat16).astype(jnp.float32)

    project(0)
    rotate(0, q_gain, q_rows)
    project(1)
    rotate(1, k_gain, k_rows)
    project(2)
    for h in range(heads):
        v_rows[pl.ds(h, seqs, stride=heads), :] = proj[2, :, h * head_dim:(h + 1) * head_dim]

    scale = head_dim ** -0.5
    row_iota = lax.broadcasted_iota(jnp.int32, (cache_len, heads, 1), 0)

    def attend(b):
        position = pos_ref[b]
        at = pl.ds(pl.multiple_of(b * heads, heads), heads)
        kbuf[b, position] = k_rows[at, :].astype(jnp.bfloat16)
        vbuf[b, position] = v_rows[at, :].astype(jnp.bfloat16)
        scores = jnp.sum(kbuf[b].astype(jnp.float32) * q_rows[at, :][None], axis=-1, keepdims=True) * scale
        scores = jnp.where(row_iota <= position, scores, -1e30)
        weights = jnp.exp(scores - jnp.max(scores, axis=0, keepdims=True))
        prob = (weights / jnp.sum(weights, axis=0, keepdims=True)).astype(jnp.bfloat16).astype(jnp.float32)
        mixed_rows[at, :] = jnp.sum(prob * vbuf[b].astype(jnp.float32), axis=0)

    for i in range(CACHE_BLOCKS):
        for kind in range(2):
            cache_in(kind, i).wait()

        def body(step, carry):
            for u in range(ATTEND_UNROLL):
                attend(i * block + step * ATTEND_UNROLL + u)
            return carry

        lax.fori_loop(0, block // ATTEND_UNROLL, body, 0)
        for kind in range(2):
            cache_out(kind, i).start()

    for h in range(heads):
        mixed[:, h * head_dim:(h + 1) * head_dim] = mixed_rows[pl.ds(h, seqs, stride=heads), :].astype(jnp.bfloat16)
    for c in range(chunks):
        weight_copy(3 * chunks + c).wait()
        at = slice(c * cols, (c + 1) * cols)
        added = jnp.dot(mixed[...], wbuf[3 * chunks + c], preferred_element_type=jnp.float32)
        x_out[:, at] = (x_ref[:, at].astype(jnp.float32) + added).astype(jnp.bfloat16)
    for i in range(CACHE_BLOCKS):
        for kind in range(2):
            cache_out(kind, i).wait()


def attention_local(layer, hidden, positions, cosines, sines, attn_gain, q_gain, k_gain, w_query, w_key, w_value, w_out, k_cache, v_cache, k_new, v_new):
    seqs, model = hidden.shape
    cache_shape = k_cache.shape[1:]
    heads, head_dim = cache_shape[2:]
    vmem = pl.BlockSpec(memory_space=pltpu.VMEM)
    smem = pl.BlockSpec(memory_space=pltpu.SMEM)
    hbm = pl.BlockSpec(memory_space=pl.ANY)
    operands = [positions, hidden, cosines, sines, attn_gain, q_gain, k_gain, w_query, w_key, w_value, w_out, k_cache, v_cache]
    specs = [smem] + [vmem] * 6 + [hbm] * 6
    aliases = {}
    if k_new is not None:
        aliases = {len(operands): 1, len(operands) + 1: 2}
        operands += [k_new, v_new]
        specs += [hbm, hbm]
    chunks = model // COLS
    return pl.pallas_call(
        functools.partial(attention_kernel, layer, bool(aliases)),
        out_shape=(jax.ShapeDtypeStruct(hidden.shape, hidden.dtype), jax.ShapeDtypeStruct(k_cache.shape, k_cache.dtype), jax.ShapeDtypeStruct(v_cache.shape, v_cache.dtype)),
        in_specs=specs,
        out_specs=(vmem, hbm, hbm),
        input_output_aliases=aliases,
        scratch_shapes=[
            pltpu.VMEM((4 * chunks, model, COLS), jnp.bfloat16),
            pltpu.VMEM(cache_shape, jnp.bfloat16),
            pltpu.VMEM(cache_shape, jnp.bfloat16),
            pltpu.VMEM((3, seqs, model), jnp.float32),
            pltpu.VMEM((seqs * heads, head_dim), jnp.float32),
            pltpu.VMEM((seqs * heads, head_dim), jnp.float32),
            pltpu.VMEM((seqs * heads, head_dim), jnp.float32),
            pltpu.VMEM((seqs * heads, head_dim), jnp.float32),
            pltpu.VMEM((seqs, model), jnp.bfloat16),
            pltpu.SemaphoreType.DMA((4 * chunks,)),
            pltpu.SemaphoreType.DMA((2, CACHE_BLOCKS)),
            pltpu.SemaphoreType.DMA((2, CACHE_BLOCKS)),
        ],
        compiler_params=pltpu.CompilerParams(vmem_limit_bytes=67043328),
        name='attention_layer',
    )(*operands)


def moe_kernel(groups, layer, x_ref, routes_ref, gain_ref, wr_ref, wg, wu, wd, out_ref, ring, rows, xg, act, ys, smat, meta, meta_in, part, dbuf, tbuf, f1, f2, ring_sem, ag_send, ag_recv, meta_send, meta_recv, rs_send, rs_recv):
    seqs, model = x_ref.shape
    local_experts = wg.shape[0]
    experts = wr_ref.shape[1]
    ffn = wg.shape[2]
    slots = xg.shape[1] // groups
    chips = groups // 2
    me = lax.axis_index('ep')
    chip, core = me // 2, me % 2
    step = 1 - 2 * core
    partner = chip * 2 + 1 - core

    def device(offset, core_idx):
        return ((chip + offset + chips) % chips) * 2 + core_idx

    long_dev, short_dev, far_dev = device(step, core), device(-step, core), device(2 * step, core)
    gate_units = 2 * model // UNIT
    down_units = model // UNIT
    total_gate = gate_units * local_experts

    def gate_copy(expert, j):
        weights = wg if j < gate_units // 2 else wu
        slot = (expert * gate_units + j) % RING
        return pltpu.make_async_copy(weights.at[expert, pl.ds((j % (gate_units // 2)) * UNIT, UNIT), :], ring.at[slot], ring_sem.at[slot])

    def down_slot(unit):
        return (total_gate + unit) % RING

    def down_copy(unit):
        half, expert = unit // local_experts, unit % local_experts
        slot = down_slot(unit)
        return pltpu.make_async_copy(wd.at[expert, :, pl.ds(pl.multiple_of(half * UNIT, UNIT), UNIT)], ring.at[slot], ring_sem.at[slot])

    ahead = RING // gate_units
    for expert in range(ahead):
        for j in range(gate_units):
            gate_copy(expert, j).start()

    barrier = pltpu.get_barrier_semaphore()
    for j in range(1, groups):
        pl.semaphore_signal(barrier, inc=1, device_id={'ep': (me + j) % groups}, device_id_type=MESH)

    values = x_ref[...].astype(jnp.float32)
    inv_rms = lax.rsqrt(jnp.mean(values * values, axis=-1, keepdims=True) + RMS_EPS)
    normed = (values * inv_rms * gain_ref[layer:layer + 1, :]).astype(jnp.bfloat16)
    rows[me] = normed
    pl.semaphore_wait(barrier, groups - 1)

    part_rows = seqs // AG_PARTS

    def rows_copy(role, source, peer, q):
        ref = rows.at[source, pl.ds(q * part_rows, part_rows), :]
        return pltpu.make_async_remote_copy(src_ref=ref, dst_ref=ref, send_sem=ag_send.at[role, q], recv_sem=ag_recv.at[role, q], device_id={'ep': peer}, device_id_type=MESH)

    plan = [(me, partner), (me, long_dev), (me, short_dev), (short_dev, long_dev), (short_dev, partner), (long_dev, partner), (far_dev, partner)]
    copies = [[rows_copy(role, source, peer, q) for q in range(AG_PARTS)] for role, (source, peer) in enumerate(plan)]
    for q in range(AG_PARTS):
        for role in (1, 2, 0):
            copies[role][q].start()

    logits = jnp.dot(normed, wr_ref[...], preferred_element_type=jnp.float32)
    shifted = jnp.exp(logits - jnp.max(logits, axis=-1, keepdims=True))
    prob = shifted / jnp.sum(shifted, axis=-1, keepdims=True)
    expert_iota = lax.broadcasted_iota(jnp.int32, (seqs, experts), 1)
    routes = routes_ref[layer]
    chosen = expert_iota == routes[:, 0:1]
    for j in range(1, routes.shape[1]):
        chosen = chosen | (expert_iota == routes[:, j:j + 1])
    row_iota = lax.broadcasted_iota(jnp.int32, (seqs, seqs), 0)
    col_iota = lax.broadcasted_iota(jnp.int32, (seqs, seqs), 1)
    lower = jnp.where(col_iota < row_iota, 1.0, 0.0).astype(jnp.bfloat16)
    ranks = jnp.dot(lower, jnp.where(chosen, 1.0, 0.0).astype(jnp.bfloat16), preferred_element_type=jnp.float32)
    ranks = jnp.where(chosen, ranks, -1.0)
    gates = jnp.where(chosen, prob, 0.0)
    both = jnp.concatenate([jnp.concatenate([ranks, gates], axis=1), jnp.zeros((2 * experts - seqs, 2 * experts), jnp.float32)], axis=0)
    both_t = both.T
    meta[:, :2 * experts] = both_t[:experts]
    meta[:, 2 * experts:] = both_t[experts:]

    def meta_copy(j):
        peer = (me + j) % groups
        return pltpu.make_async_remote_copy(src_ref=meta.at[pl.ds(pl.multiple_of(peer * local_experts, local_experts), local_experts), :], dst_ref=meta_in.at[me], send_sem=meta_send.at[j], recv_sem=meta_recv.at[j], device_id={'ep': peer}, device_id_type=MESH)

    meta_copies = [meta_copy(j) for j in range(1, groups)]
    meta_in[me] = meta[pl.ds(pl.multiple_of(me * local_experts, local_experts), local_experts), :]
    for copy in meta_copies:
        copy.start()

    def gather(source):
        info = meta_in[source]
        rank = info[:, :2 * experts].reshape(local_experts, 1, 2 * experts)
        gate = info[:, 2 * experts:].reshape(local_experts, 1, 2 * experts)
        place = lax.broadcasted_iota(jnp.int32, (local_experts, slots, 2 * experts), 1).astype(jnp.float32)
        hit = jnp.broadcast_to(rank, place.shape) == place
        total = local_experts * slots
        onehot = jnp.where(hit, 1.0, 0.0).reshape(total, 2 * experts)[:, :seqs].astype(jnp.bfloat16)
        taken = jnp.dot(onehot, rows[source], preferred_element_type=jnp.float32).astype(jnp.bfloat16)
        at = pl.ds(pl.multiple_of(source * slots, slots), slots)
        for e in range(local_experts):
            xg[e, at, :] = taken[e * slots:(e + 1) * slots]
        weight = jnp.where(hit, jnp.broadcast_to(gate, place.shape), 0.0).reshape(total, 2 * experts).T[:seqs]
        first = weight.astype(jnp.bfloat16)
        rest = weight - first.astype(jnp.float32)
        second = rest.astype(jnp.bfloat16)
        third = (rest - second.astype(jnp.float32)).astype(jnp.bfloat16)
        smat[source, pl.ds(0, seqs), :] = first
        smat[source, pl.ds(seqs, seqs), :] = second
        smat[source, pl.ds(2 * seqs, seqs), :] = third

    gather(me)
    for q in range(AG_PARTS):
        copies[1][q].wait_recv()
        copies[3][q].start()
        copies[4][q].start()
        copies[2][q].wait_recv()
        copies[5][q].start()
    for copy in meta_copies:
        copy.wait_recv()
    for q in range(AG_PARTS):
        copies[0][q].wait_recv()
    gather(partner)
    gather(short_dev)
    gather(long_dev)
    for role in (4, 5):
        for q in range(AG_PARTS):
            copies[role][q].wait_recv()
    gather(device(step, 1 - core))
    gather(device(-step, 1 - core))
    for q in range(AG_PARTS):
        copies[3][q].wait_recv()
        copies[6][q].start()
    gather(far_dev)
    for q in range(AG_PARTS):
        copies[6][q].wait_recv()
    gather(device(2 * step, 1 - core))

    def expert_body(e, carry):
        def product(first):
            total = None
            for j in range(gate_units // 2):
                slot = (e * gate_units + first + j) % RING
                gate_copy(e, first + j).wait()
                term = jnp.dot(xg[e, :, pl.ds(j * UNIT, UNIT)], ring[slot], preferred_element_type=jnp.float32)
                total = term if total is None else total + term
            return total

        gate_act = product(0)
        up_act = product(gate_units // 2)
        act[e] = (jax.nn.silu(gate_act) * up_act).astype(jnp.bfloat16)

        @pl.when(e + ahead < local_experts)
        def _():
            for j in range(gate_units):
                gate_copy(e + ahead, j).start()

        first_unit = (e + ahead - local_experts) * gate_units

        @pl.when((first_unit >= 0) & (first_unit < down_units * local_experts))
        def _():
            for j in range(gate_units):
                down_copy(first_unit + j).start()

        return carry

    lax.fori_loop(0, local_experts, expert_body, 0)

    width = model // RS_CHUNKS
    per_unit = UNIT // width

    def rs_copy(role, k, source, target, peer):
        return pltpu.make_async_remote_copy(src_ref=source, dst_ref=target, send_sem=rs_send.at[role, k], recv_sem=rs_recv.at[role, k], device_id={'ep': peer}, device_id_type=MESH)

    far_chip, long_chip, short_chip = far_dev // 2, long_dev // 2, short_dev // 2

    def pair_copy(k):
        return rs_copy(0, k, part.at[k, 1 - core], dbuf.at[k], partner)

    def far_copy(k):
        return rs_copy(1, k, part.at[k, core, far_chip], tbuf.at[k], long_dev)

    def short_copy(k):
        return rs_copy(2, k, part.at[k, core, short_chip], f1.at[k], short_dev)

    def long_copy(k):
        return rs_copy(3, k, part.at[k, core, long_chip], f2.at[k], long_dev)

    def compute_chunk(k):
        half = k // per_unit
        column = (k % per_unit) * width

        def down_body(i, carry):
            for u in range(4):
                e = i * 4 + u
                unit = half * local_experts + e
                slot = down_slot(unit)
                if k % per_unit == 0:
                    down_copy(unit).wait()
                out = jnp.dot(act[e], ring[slot, :, pl.ds(column, width)], preferred_element_type=jnp.float32).astype(jnp.bfloat16)
                at = pl.ds(pl.multiple_of(e * slots, slots), slots)
                for b in range(groups):
                    ys[b, at, :] = out[b * slots:(b + 1) * slots]
            return carry

        lax.fori_loop(0, local_experts // 4, down_body, 0)
        for b in range(groups):
            sums = jnp.dot(smat[b], ys[b], preferred_element_type=jnp.float32)
            part[k, b % 2, b // 2] = sums[:seqs] + sums[seqs:2 * seqs] + sums[2 * seqs:]

    def pair_sum(k):
        pair_copy(k).wait_recv()
        part[k, core] = part[k, core] + dbuf[k]
        far_copy(k).start()
        short_copy(k).start()

    def forward(k):
        far_copy(k).wait_recv()
        part[k, core, long_chip] = part[k, core, long_chip] + tbuf[k]
        long_copy(k).start()

    def finish(k):
        short_copy(k).wait_recv()
        long_copy(k).wait_recv()
        moe_out = part[k, core, chip] + f1[k] + f2[k]
        at = pl.ds(k * width, width)
        out_ref[:, at] = (x_ref[:, at].astype(jnp.float32) + moe_out).astype(jnp.bfloat16)

    for k in range(RS_CHUNKS):
        compute_chunk(k)
        pair_copy(k).start()
        if k >= 1:
            pair_sum(k - 1)
        if k >= 2:
            forward(k - 2)
    pair_sum(RS_CHUNKS - 1)
    for k in range(RS_CHUNKS - 2, RS_CHUNKS):
        forward(k)
    for k in range(RS_CHUNKS):
        finish(k)
    for group in copies:
        for copy in group:
            copy.wait_send()
    for copy in meta_copies:
        copy.wait_send()
    for k in range(RS_CHUNKS):
        for make in (pair_copy, far_copy, short_copy, long_copy):
            make(k).wait_send()


def moe_local(hidden, routes, mlp_gain, w_router, w_gate, w_up, w_down, groups, layer):
    seqs, model = hidden.shape
    experts = w_router.shape[1]
    local_experts, _, ffn = w_gate.shape
    slots = CAP_FACTOR * seqs * routes.shape[2] // experts
    chips = groups // 2
    width = model // RS_CHUNKS
    vmem = pl.BlockSpec(memory_space=pltpu.VMEM)
    hbm = pl.BlockSpec(memory_space=pl.ANY)
    return pl.pallas_call(
        functools.partial(moe_kernel, groups, layer),
        out_shape=jax.ShapeDtypeStruct((seqs, model), jnp.bfloat16),
        in_specs=[vmem, vmem, vmem, vmem, hbm, hbm, hbm],
        out_specs=vmem,
        scratch_shapes=[
            pltpu.VMEM((RING, UNIT, ffn), jnp.bfloat16),
            pltpu.VMEM((groups, seqs, model), jnp.bfloat16),
            pltpu.VMEM((local_experts, groups * slots, model), jnp.bfloat16),
            pltpu.VMEM((local_experts, groups * slots, ffn), jnp.bfloat16),
            pltpu.VMEM((groups, local_experts * slots, width), jnp.bfloat16),
            pltpu.VMEM((groups, 3 * seqs, local_experts * slots), jnp.bfloat16),
            pltpu.VMEM((experts, 4 * experts), jnp.float32),
            pltpu.VMEM((groups, local_experts, 4 * experts), jnp.float32),
            pltpu.VMEM((RS_CHUNKS, 2, chips, seqs, width), jnp.float32),
            pltpu.VMEM((RS_CHUNKS, chips, seqs, width), jnp.float32),
            pltpu.VMEM((RS_CHUNKS, seqs, width), jnp.float32),
            pltpu.VMEM((RS_CHUNKS, seqs, width), jnp.float32),
            pltpu.VMEM((RS_CHUNKS, seqs, width), jnp.float32),
            pltpu.SemaphoreType.DMA((RING,)),
            pltpu.SemaphoreType.DMA((7, AG_PARTS)),
            pltpu.SemaphoreType.DMA((7, AG_PARTS)),
            pltpu.SemaphoreType.DMA((groups,)),
            pltpu.SemaphoreType.DMA((groups,)),
            pltpu.SemaphoreType.DMA((4, RS_CHUNKS)),
            pltpu.SemaphoreType.DMA((4, RS_CHUNKS)),
        ],
        compiler_params=pltpu.CompilerParams(collective_id=layer, has_side_effects=True, vmem_limit_bytes=67043328),
        name='moe_layer',
    )(hidden, routes, mlp_gain, w_router, w_gate, w_up, w_down)


def solution(mesh):
    groups = mesh.shape['ep']
    batch_axes = ('dp', 'ep')

    def device_step(hidden, positions, expert_ids, k_cache, v_cache, w_query, w_key, w_value, w_out, attn_gain, q_gain, k_gain, mlp_gain, w_router, w_gate, w_up, w_down):
        cosines, sines = rope_tables(positions, k_cache.shape[4])
        k_new, v_new = None, None
        for layer in range(expert_ids.shape[0]):
            hidden, k_new, v_new = attention_local(layer, hidden, positions, cosines, sines, attn_gain, q_gain, k_gain, w_query, w_key, w_value, w_out, k_cache, v_cache, k_new, v_new)
            hidden = moe_local(hidden, expert_ids, mlp_gain, w_router, w_gate, w_up, w_down, groups, layer)
        return hidden, k_new, v_new

    row_spec = P(batch_axes, None)
    cache_spec = P(None, batch_axes, None, None, None)
    full_spec = P()
    expert_spec = P('ep', None, None)
    in_specs = (row_spec, P(batch_axes), P(None, batch_axes, None), cache_spec, cache_spec, full_spec, full_spec, full_spec, full_spec, full_spec, full_spec, full_spec, full_spec, full_spec, expert_spec, expert_spec, expert_spec)
    return jax.shard_map(device_step, mesh=mesh, in_specs=in_specs, out_specs=(row_spec, cache_spec, cache_spec), check_vma=False)
```

profile of v0, /device:TPU:113, one launch (start us, length us, event | category | flops | bytes accessed | tf_op | source)
XLA Modules:
  0.0 166.0 jit_solution(1355312666639378735)
XLA Ops:
  0.6 0.7 convert_element_type.3
  1.3 1.4 copy.22.routes_ref
  2.7 0.2 fusion
  2.9 0.7 pad_maximum_fusion
  3.6 1.9 %copy.23.wr_ref = bf16[2048,64]{1,0:T(8,128)(2,1)} copy(bf16[2048,64]{0,1:T(8,128)(2,1)} %param.30) | data formatting | bytes 524288 | tf_op args[13]
  5.6 19.3 %attention_layer.2 = (bf16[64,2048]{1,0:T(8,128)(2,1)}, bf16[2,64,16,16,128]{4,3,2,1,0:T(8,128)(2,1)}, bf16[2,64,16,16,128]{4,3,2,1,0:T(8,128)(2,1)}) custom-call(s32[64]{0:T(128)} %pos_ref.3, bf16[64,2048]{1,0:T(8,128)(2,1)} %x_ref.1, f32[64,128]{1,0:T(8,128)} %get-tuple-element.18.cos_ref, f32[64,128]{1,0:T(8,128)} %get-tuple-element.19.sin_ref, ...), custom_call_target="tpu_custom_call" | custom-call | tf_op jit(solution)/shard_map/attention_layer/pallas_call | solution.py:147
  24.9 60.5 %moe_layer.2.x_ref = bf16[64,2048]{1,0:T(8,128)(2,1)} custom-call(bf16[64,2048]{1,0:T(8,128)(2,1)} %get-tuple-element.9.x_ref, s32[2,64,8]{2,1,0:T(8,128)} %copy.22.routes_ref, f32[2,2048]{1,0:T(2,128)} %gain_ref.3, bf16[2048,64]{1,0:T(8,128)(2,1)} %copy.23.wr_ref, bf16[8,2048,1024]{2,1,0:T(8,128)(2,1)} %wg.3, bf16[8,2048,1024]{2,1,0:T(8,128)(2,1)} %wu.3, ...), custom_call_target="tpu_custom_call" | custom-call | tf_op jit(solution)/shard_map/moe_layer/pallas_call | solution.py:429
  85.4 19.2 %attention_layer.3 = (bf16[64,2048]{1,0:T(8,128)(2,1)}, bf16[2,64,16,16,128]{4,3,2,1,0:T(8,128)(2,1)}, bf16[2,64,16,16,128]{4,3,2,1,0:T(8,128)(2,1)}) custom-call(s32[64]{0:T(128)} %pos_ref.3, bf16[64,2048]{1,0:T(8,128)(2,1)} %moe_layer.2.x_ref, f32[64,128]{1,0:T(8,128)} %get-tuple-element.18.cos_ref, ...), custom_call_target="tpu_custom_call", output_to_operand_aliasing={{1}: (13, {}), {2}: (14, {})} | custom-call | tf_op jit(solution)/shard_map/attention_layer/pallas_call | solution.py:147
  104.6 59.8 %moe_layer.3 = bf16[64,2048]{1,0:T(8,128)(2,1)} custom-call(bf16[64,2048]{1,0:T(8,128)(2,1)} %get-tuple-element.12.x_ref, s32[2,64,8]{2,1,0:T(8,128)} %copy.22.routes_ref, f32[2,2048]{1,0:T(2,128)} %gain_ref.3, bf16[2048,64]{1,0:T(8,128)(2,1)} %copy.23.wr_ref, bf16[8,2048,1024]{2,1,0:T(8,128)(2,1)} %wg.3, bf16[8,2048,1024]{2,1,0:T(8,128)(2,1)} %wu.3, ...), custom_call_target="tpu_custom_call" | custom-call | tf_op jit(solution)/shard_map/moe_layer/pallas_call | solution.py:429
  164.3 1.7 %copy.29 = bf16[64,2048]{1,0:T(8,128)(2,1)} copy(bf16[64,2048]{1,0:T(8,128)(2,1)} %moe_layer.3) | data formatting | bytes 524288
  (1 shorter events, 0.0 us)
where the time goes:
time: 166 us
  Pallas kernels  159 us (96%)
  local copies, waits for them, and re-layouts  5.04 us (3%)
    pallas_call x2, Pallas kernels, moe_local(): pl.pallas_call(functools.partial(moe_kernel, groups, layer), out_shape=ja...  120 us
    pallas_call x2, Pallas kernels, attention_local(): pl.pallas_call(functools.partial(attention_kernel, layer, bool(aliases)),...  38.5 us
    unnamed x3, local copies, waits for them, and re-layouts  5.04 us

commit v1 on v0

--- a/solution.py
+++ b/solution.py
@@ -2,6 +2,7 @@
 
 import jax
 import jax.numpy as jnp
+import numpy as np
 from jax import lax
 from jax.experimental import pallas as pl
 from jax.experimental.pallas import tpu as pltpu
@@ -12,12 +13,14 @@
 CAP_FACTOR = 2
 MESH = pl.DeviceIdType.MESH
 AG_PARTS = 2
-RS_CHUNKS = 4
+RS_CHUNKS = 8
 UNIT = 1024
 RING = 20
+LANES = 128
+FORWARD_LAG = 5
 COLS = 512
 CACHE_BLOCKS = 4
-ATTEND_UNROLL = 4
+ATTEND_UNROLL = 8
 
 
 def rms_norm(values, gain_vec):
@@ -26,17 +29,17 @@
     return values * inv_rms * gain_vec.astype(jnp.float32)
 
 
-def rope_tables(positions, head_dim):
+def rope_table(length, head_dim):
     half_dim = head_dim // 2
-    frequencies = ROPE_BASE ** (-jnp.arange(half_dim, dtype=jnp.float32) / half_dim)
-    angles = positions.astype(jnp.float32)[:, None] * frequencies[None, :]
-    cosines, sines = jnp.cos(angles), jnp.sin(angles)
-    return jnp.concatenate([cosines, cosines], axis=1), jnp.concatenate([-sines, sines], axis=1)
-
-
-def attention_kernel(layer, aliased, pos_ref, x_ref, cos_ref, sin_ref, attn_gain, q_gain, k_gain, wq, wk, wv, wo, k_in, v_in, *rest):
+    frequencies = np.float32(ROPE_BASE) ** (-np.arange(half_dim, dtype=np.float32) / np.float32(half_dim))
+    angles = np.arange(length, dtype=np.float32)[:, None] * frequencies[None, :]
+    cosines, sines = np.cos(angles), np.sin(angles)
+    return np.concatenate([np.concatenate([cosines, cosines], axis=1), np.concatenate([-sines, sines], axis=1)], axis=0).astype(np.float32)
+
+
+def attention_kernel(layer, aliased, pos_ref, x_ref, table_ref, attn_gain, q_gain, k_gain, wq, wk, wv, wo, k_in, v_in, *rest):
     rest = rest[2:] if aliased else rest
-    x_out, k_out, v_out, wbuf, kbuf, vbuf, proj, q_rows, k_rows, v_rows, mixed_rows, mixed, w_sem, in_sem, out_sem = rest
+    x_out, k_out, v_out, wbuf, kbuf, vbuf, proj, q_rows, k_rows, v_rows, mixed_rows, mixed, cos_ref, sin_ref, w_sem, in_sem, out_sem = rest
     seqs, model = x_ref.shape
     cache_len, heads, head_dim = kbuf.shape[1:]
     cols = wbuf.shape[2]
@@ -65,11 +68,17 @@
     for index in range(3 * chunks, 4 * chunks):
         weight_copy(index).start()
 
+    for b in range(seqs):
+        position = pos_ref[b]
+        cos_ref[b:b + 1, :] = table_ref[pl.ds(position, 1), :]
+        sin_ref[b:b + 1, :] = table_ref[pl.ds(position + cache_len, 1), :]
     normed = rms_norm(x_ref[...], attn_gain[layer:layer + 1, :]).astype(jnp.bfloat16)
 
     def project(kind):
         for c in range(chunks):
-            weight_copy(kind * chunks + c).wait()
+            if c % 2 == 0:
+                weight_copy(kind * chunks + c).wait()
+                weight_copy(kind * chunks + c + 1).wait()
             proj[kind, :, c * cols:(c + 1) * cols] = jnp.dot(normed, wbuf[kind * chunks + c], preferred_element_type=jnp.float32)
 
     def rotate(kind, gain, target):
@@ -121,6 +130,7 @@
         mixed[:, h * head_dim:(h + 1) * head_dim] = mixed_rows[pl.ds(h, seqs, stride=heads), :].astype(jnp.bfloat16)
     for c in range(chunks):
         weight_copy(3 * chunks + c).wait()
+    for c in range(chunks):
         at = slice(c * cols, (c + 1) * cols)
         added = jnp.dot(mixed[...], wbuf[3 * chunks + c], preferred_element_type=jnp.float32)
         x_out[:, at] = (x_ref[:, at].astype(jnp.float32) + added).astype(jnp.bfloat16)
@@ -129,15 +139,15 @@
             cache_out(kind, i).wait()
 
 
-def attention_local(layer, hidden, positions, cosines, sines, attn_gain, q_gain, k_gain, w_query, w_key, w_value, w_out, k_cache, v_cache, k_new, v_new):
+def attention_local(layer, hidden, positions, table, attn_gain, q_gain, k_gain, w_query, w_key, w_value, w_out, k_cache, v_cache, k_new, v_new):
     seqs, model = hidden.shape
     cache_shape = k_cache.shape[1:]
     heads, head_dim = cache_shape[2:]
     vmem = pl.BlockSpec(memory_space=pltpu.VMEM)
     smem = pl.BlockSpec(memory_space=pltpu.SMEM)
     hbm = pl.BlockSpec(memory_space=pl.ANY)
-    operands = [positions, hidden, cosines, sines, attn_gain, q_gain, k_gain, w_query, w_key, w_value, w_out, k_cache, v_cache]
-    specs = [smem] + [vmem] * 6 + [hbm] * 6
+    operands = [positions, hidden, table, attn_gain, q_gain, k_gain, w_query, w_key, w_value, w_out, k_cache, v_cache]
+    specs = [smem] + [vmem] * 5 + [hbm] * 6
     aliases = {}
     if k_new is not None:
         aliases = {len(operands): 1, len(operands) + 1: 2}
@@ -160,6 +170,8 @@
             pltpu.VMEM((seqs * heads, head_dim), jnp.float32),
             pltpu.VMEM((seqs * heads, head_dim), jnp.float32),
             pltpu.VMEM((seqs, model), jnp.bfloat16),
+            pltpu.VMEM((seqs, head_dim), jnp.float32),
+            pltpu.VMEM((seqs, head_dim), jnp.float32),
             pltpu.SemaphoreType.DMA((4 * chunks,)),
             pltpu.SemaphoreType.DMA((2, CACHE_BLOCKS)),
             pltpu.SemaphoreType.DMA((2, CACHE_BLOCKS)),
@@ -169,10 +181,10 @@
     )(*operands)
 
 
-def moe_kernel(groups, layer, x_ref, routes_ref, gain_ref, wr_ref, wg, wu, wd, out_ref, ring, rows, xg, act, ys, smat, meta, meta_in, part, dbuf, tbuf, f1, f2, ring_sem, ag_send, ag_recv, meta_send, meta_recv, rs_send, rs_recv):
+def moe_kernel(groups, layer, x_ref, routes_ref, gain_ref, wr_ref, wg, wu, wd, out_ref, ring, rows, xg, act, ys, smat, meta, meta_in, part, dbuf, tbuf, f1, f2, ring_sem, down_sem, ag_send, ag_recv, meta_send, meta_recv, rs_send, rs_recv):
     seqs, model = x_ref.shape
     local_experts = wg.shape[0]
-    experts = wr_ref.shape[1]
+    experts = wr_ref.shape[0]
     ffn = wg.shape[2]
     slots = xg.shape[1] // groups
     chips = groups // 2
@@ -188,6 +200,8 @@
     gate_units = 2 * model // UNIT
     down_units = model // UNIT
     total_gate = gate_units * local_experts
+    width = model // RS_CHUNKS
+    per_unit = UNIT // width
 
     def gate_copy(expert, j):
         weights = wg if j < gate_units // 2 else wu
@@ -197,10 +211,10 @@
     def down_slot(unit):
         return (total_gate + unit) % RING
 
-    def down_copy(unit):
+    def down_copy(unit, c):
         half, expert = unit // local_experts, unit % local_experts
         slot = down_slot(unit)
-        return pltpu.make_async_copy(wd.at[expert, :, pl.ds(pl.multiple_of(half * UNIT, UNIT), UNIT)], ring.at[slot], ring_sem.at[slot])
+        return pltpu.make_async_copy(wd.at[expert, :, pl.ds(half * UNIT + c * width, width)], ring.at[slot, :, pl.ds(c * width, width)], down_sem.at[unit, c])
 
     ahead = RING // gate_units
     for expert in range(ahead):
@@ -229,24 +243,21 @@
         for role in (1, 2, 0):
             copies[role][q].start()
 
-    logits = jnp.dot(normed, wr_ref[...], preferred_element_type=jnp.float32)
-    shifted = jnp.exp(logits - jnp.max(logits, axis=-1, keepdims=True))
-    prob = shifted / jnp.sum(shifted, axis=-1, keepdims=True)
-    expert_iota = lax.broadcasted_iota(jnp.int32, (seqs, experts), 1)
+    logits = lax.dot_general(wr_ref[...], normed, (((1,), (1,)), ((), ())), preferred_element_type=jnp.float32)
+    shifted = jnp.exp(logits - jnp.max(logits, axis=0, keepdims=True))
+    prob = shifted / jnp.sum(shifted, axis=0, keepdims=True)
+    expert_iota = lax.broadcasted_iota(jnp.int32, (experts, seqs), 0)
     routes = routes_ref[layer]
-    chosen = expert_iota == routes[:, 0:1]
-    for j in range(1, routes.shape[1]):
-        chosen = chosen | (expert_iota == routes[:, j:j + 1])
+    chosen = expert_iota == routes[0:1, :]
+    for j in range(1, routes.shape[0]):
+        chosen = chosen | (expert_iota == routes[j:j + 1, :])
     row_iota = lax.broadcasted_iota(jnp.int32, (seqs, seqs), 0)
     col_iota = lax.broadcasted_iota(jnp.int32, (seqs, seqs), 1)
-    lower = jnp.where(col_iota < row_iota, 1.0, 0.0).astype(jnp.bfloat16)
-    ranks = jnp.dot(lower, jnp.where(chosen, 1.0, 0.0).astype(jnp.bfloat16), preferred_element_type=jnp.float32)
-    ranks = jnp.where(chosen, ranks, -1.0)
-    gates = jnp.where(chosen, prob, 0.0)
-    both = jnp.concatenate([jnp.concatenate([ranks, gates], axis=1), jnp.zeros((2 * experts - seqs, 2 * experts), jnp.float32)], axis=0)
-    both_t = both.T
-    meta[:, :2 * experts] = both_t[:experts]
-    meta[:, 2 * experts:] = both_t[experts:]
+    upper = jnp.where(row_iota < col_iota, 1.0, 0.0).astype(jnp.bfloat16)
+    ranks = jnp.dot(jnp.where(chosen, 1.0, 0.0).astype(jnp.bfloat16), upper, preferred_element_type=jnp.float32)
+    fill = jnp.zeros((experts, LANES - seqs), jnp.float32)
+    meta[:, :LANES] = jnp.concatenate([jnp.where(chosen, ranks, -1.0), fill - 1.0], axis=1)
+    meta[:, LANES:] = jnp.concatenate([jnp.where(chosen, prob, 0.0), fill], axis=1)
 
     def meta_copy(j):
         peer = (me + j) % groups
@@ -259,17 +270,17 @@
 
     def gather(source):
         info = meta_in[source]
-        rank = info[:, :2 * experts].reshape(local_experts, 1, 2 * experts)
-        gate = info[:, 2 * experts:].reshape(local_experts, 1, 2 * experts)
-        place = lax.broadcasted_iota(jnp.int32, (local_experts, slots, 2 * experts), 1).astype(jnp.float32)
+        rank = info[:, :LANES].reshape(local_experts, 1, LANES)
+        gate = info[:, LANES:].reshape(local_experts, 1, LANES)
+        place = lax.broadcasted_iota(jnp.int32, (local_experts, slots, LANES), 1).astype(jnp.float32)
         hit = jnp.broadcast_to(rank, place.shape) == place
         total = local_experts * slots
-        onehot = jnp.where(hit, 1.0, 0.0).reshape(total, 2 * experts)[:, :seqs].astype(jnp.bfloat16)
+        onehot = jnp.where(hit, 1.0, 0.0).reshape(total, LANES)[:, :seqs].astype(jnp.bfloat16)
         taken = jnp.dot(onehot, rows[source], preferred_element_type=jnp.float32).astype(jnp.bfloat16)
         at = pl.ds(pl.multiple_of(source * slots, slots), slots)
         for e in range(local_experts):
             xg[e, at, :] = taken[e * slots:(e + 1) * slots]
-        weight = jnp.where(hit, jnp.broadcast_to(gate, place.shape), 0.0).reshape(total, 2 * experts).T[:seqs]
+        weight = jnp.where(hit, jnp.broadcast_to(gate, place.shape), 0.0).reshape(total, LANES).T[:seqs]
         first = weight.astype(jnp.bfloat16)
         rest = weight - first.astype(jnp.float32)
         second = rest.astype(jnp.bfloat16)
@@ -306,11 +317,13 @@
     gather(device(2 * step, 1 - core))
 
     def expert_body(e, carry):
+        for j in range(gate_units):
+            gate_copy(e, j).wait()
+
         def product(first):
             total = None
             for j in range(gate_units // 2):
                 slot = (e * gate_units + first + j) % RING
-                gate_copy(e, first + j).wait()
                 term = jnp.dot(xg[e, :, pl.ds(j * UNIT, UNIT)], ring[slot], preferred_element_type=jnp.float32)
                 total = term if total is None else total + term
             return total
@@ -324,19 +337,18 @@
             for j in range(gate_units):
                 gate_copy(e + ahead, j).start()
 
-        first_unit = (e + ahead - local_experts) * gate_units
-
-        @pl.when((first_unit >= 0) & (first_unit < down_units * local_experts))
-        def _():
-            for j in range(gate_units):
-                down_copy(first_unit + j).start()
+        for half in range(down_units):
+            freed = (half + 1) * local_experts // gate_units + local_experts - ahead - 1
+
+            @pl.when(e == freed)
+            def _():
+                for c in range(per_unit):
+                    for expert in range(local_experts):
+                        down_copy(half * local_experts + expert, c).start()
 
         return carry
 
     lax.fori_loop(0, local_experts, expert_body, 0)
-
-    width = model // RS_CHUNKS
-    per_unit = UNIT // width
 
     def rs_copy(role, k, source, target, peer):
         return pltpu.make_async_remote_copy(src_ref=source, dst_ref=target, send_sem=rs_send.at[role, k], recv_sem=rs_recv.at[role, k], device_id={'ep': peer}, device_id_type=MESH)
@@ -359,20 +371,13 @@
         half = k // per_unit
         column = (k % per_unit) * width
 
-        def down_body(i, carry):
-            for u in range(4):
-                e = i * 4 + u
-                unit = half * local_experts + e
-                slot = down_slot(unit)
-                if k % per_unit == 0:
-                    down_copy(unit).wait()
-                out = jnp.dot(act[e], ring[slot, :, pl.ds(column, width)], preferred_element_type=jnp.float32).astype(jnp.bfloat16)
-                at = pl.ds(pl.multiple_of(e * slots, slots), slots)
-                for b in range(groups):
-                    ys[b, at, :] = out[b * slots:(b + 1) * slots]
-            return carry
-
-        lax.fori_loop(0, local_experts // 4, down_body, 0)
+        units = [half * local_experts + e for e in range(local_experts)]
+        for unit in units:
+            down_copy(unit, k % per_unit).wait()
+        for e, unit in enumerate(units):
+            out = jnp.dot(act[e], ring[down_slot(unit), :, column:column + width], preferred_element_type=jnp.float32).astype(jnp.bfloat16)
+            for b in range(groups):
+                ys[b, e * slots:(e + 1) * slots, :] = out[b * slots:(b + 1) * slots]
         for b in range(groups):
             sums = jnp.dot(smat[b], ys[b], preferred_element_type=jnp.float32)
             part[k, b % 2, b // 2] = sums[:seqs] + sums[seqs:2 * seqs] + sums[2 * seqs:]
@@ -400,10 +405,10 @@
         pair_copy(k).start()
         if k >= 1:
             pair_sum(k - 1)
-        if k >= 2:
-            forward(k - 2)
+        if k >= FORWARD_LAG:
+            forward(k - FORWARD_LAG)
     pair_sum(RS_CHUNKS - 1)
-    for k in range(RS_CHUNKS - 2, RS_CHUNKS):
+    for k in range(RS_CHUNKS - FORWARD_LAG, RS_CHUNKS):
         forward(k)
     for k in range(RS_CHUNKS):
         finish(k)
@@ -419,9 +424,9 @@
 
 def moe_local(hidden, routes, mlp_gain, w_router, w_gate, w_up, w_down, groups, layer):
     seqs, model = hidden.shape
-    experts = w_router.shape[1]
+    experts = w_router.shape[0]
     local_experts, _, ffn = w_gate.shape
-    slots = CAP_FACTOR * seqs * routes.shape[2] // experts
+    slots = CAP_FACTOR * seqs * routes.shape[1] // experts
     chips = groups // 2
     width = model // RS_CHUNKS
     vmem = pl.BlockSpec(memory_space=pltpu.VMEM)
@@ -438,14 +443,15 @@
             pltpu.VMEM((local_experts, groups * slots, ffn), jnp.bfloat16),
             pltpu.VMEM((groups, local_experts * slots, width), jnp.bfloat16),
             pltpu.VMEM((groups, 3 * seqs, local_experts * slots), jnp.bfloat16),
-            pltpu.VMEM((experts, 4 * experts), jnp.float32),
-            pltpu.VMEM((groups, local_experts, 4 * experts), jnp.float32),
+            pltpu.VMEM((experts, 2 * LANES), jnp.float32),
+            pltpu.VMEM((groups, local_experts, 2 * LANES), jnp.float32),
             pltpu.VMEM((RS_CHUNKS, 2, chips, seqs, width), jnp.float32),
             pltpu.VMEM((RS_CHUNKS, chips, seqs, width), jnp.float32),
             pltpu.VMEM((RS_CHUNKS, seqs, width), jnp.float32),
             pltpu.VMEM((RS_CHUNKS, seqs, width), jnp.float32),
             pltpu.VMEM((RS_CHUNKS, seqs, width), jnp.float32),
             pltpu.SemaphoreType.DMA((RING,)),
+            pltpu.SemaphoreType.DMA((model // UNIT * local_experts, UNIT // width)),
             pltpu.SemaphoreType.DMA((7, AG_PARTS)),
             pltpu.SemaphoreType.DMA((7, AG_PARTS)),
             pltpu.SemaphoreType.DMA((groups,)),
@@ -463,11 +469,13 @@
     batch_axes = ('dp', 'ep')
 
     def device_step(hidden, positions, expert_ids, k_cache, v_cache, w_query, w_key, w_value, w_out, attn_gain, q_gain, k_gain, mlp_gain, w_router, w_gate, w_up, w_down):
-        cosines, sines = rope_tables(positions, k_cache.shape[4])
+        table = jnp.asarray(rope_table(k_cache.shape[2], k_cache.shape[4]))
+        routes = jnp.swapaxes(expert_ids, 1, 2)
+        router = w_router.T
         k_new, v_new = None, None
         for layer in range(expert_ids.shape[0]):
-            hidden, k_new, v_new = attention_local(layer, hidden, positions, cosines, sines, attn_gain, q_gain, k_gain, w_query, w_key, w_value, w_out, k_cache, v_cache, k_new, v_new)
-            hidden = moe_local(hidden, expert_ids, mlp_gain, w_router, w_gate, w_up, w_down, groups, layer)
+            hidden, k_new, v_new = attention_local(layer, hidden, positions, table, attn_gain, q_gain, k_gain, w_query, w_key, w_value, w_out, k_cache, v_cache, k_new, v_new)
+            hidden = moe_local(hidden, routes, mlp_gain, router, w_gate, w_up, w_down, groups, layer)
         return hidden, k_new, v_new
 
     row_spec = P(batch_axes, None)

time: 166 us -> 146 us (0.88)
  Pallas kernels: 159 us -> 143 us
  local copies, waits for them, and re-layouts: 5.04 us -> 1.67 us
    pallas_call x2, Pallas kernels: 120 us -> 105 us  [moe_local(): pl.pallas_call(functools.partial(moe_kernel, groups, layer), out_shape=ja...]
    unnamed x3 -> x1, local copies, waits for them, and re-layouts: 5.04 us -> 1.67 us
where the time goes in v1:
time: 146 us
  Pallas kernels  143 us (98%)
  local copies, waits for them, and re-layouts  1.67 us (1%)
    pallas_call x2, Pallas kernels, moe_local(): pl.pallas_call(functools.partial(moe_kernel, groups, layer), out_shape=ja...  105 us
    pallas_call x2, Pallas kernels, attention_local(): pl.pallas_call(functools.partial(attention_kernel, layer, bool(aliases)),...  38.1 us

profile of v1, /device:TPU:113, one launch (start us, length us, event | category | flops | bytes accessed | tf_op | source)
XLA Modules:
  0.0 145.6 jit_solution(1632513436592708622)
XLA Ops:
  0.6 19.0 %attention_layer.2 = (bf16[64,2048]{1,0:T(8,128)(2,1)}, bf16[2,64,16,16,128]{4,3,2,1,0:T(8,128)(2,1)}, bf16[2,64,16,16,128]{4,3,2,1,0:T(8,128)(2,1)}) custom-call(s32[64]{0:T(128)} %pos_ref.3, bf16[64,2048]{1,0:T(8,128)(2,1)} %x_ref.1, f32[32,128]{1,0:T(8,128)} %constant.2.clone.table_ref, f32[2,2048]{1,0:T(2,128)} %attn_gain.3, f32[2,2048]{1,0:T(2,128)} %q_gain.3, ...), custom_call_target="tpu_custom_call" | custom-call | tf_op jit(solution)/shard_map/attention_layer/pallas_call | solution.py:157
  19.7 53.4 %moe_layer.2.x_ref = bf16[64,2048]{1,0:T(8,128)(2,1)} custom-call(bf16[64,2048]{1,0:T(8,128)(2,1)} %get-tuple-element.9.x_ref, s32[2,8,64]{2,1,0:T(8,128)} %bitcast.4, f32[2,2048]{1,0:T(2,128)} %gain_ref.3, bf16[64,2048]{1,0:T(8,128)(2,1)} %bitcast.2, bf16[8,2048,1024]{2,1,0:T(8,128)(2,1)} %wg.3, bf16[8,2048,1024]{2,1,0:T(8,128)(2,1)} %wu.3, ...), custom_call_target="tpu_custom_call" | custom-call | tf_op jit(solution)/shard_map/moe_layer/pallas_call | solution.py:434
  73.0 19.1 %attention_layer.3 = (bf16[64,2048]{1,0:T(8,128)(2,1)}, bf16[2,64,16,16,128]{4,3,2,1,0:T(8,128)(2,1)}, bf16[2,64,16,16,128]{4,3,2,1,0:T(8,128)(2,1)}) custom-call(s32[64]{0:T(128)} %pos_ref.3, bf16[64,2048]{1,0:T(8,128)(2,1)} %moe_layer.2.x_ref, f32[32,128]{1,0:T(8,128)} %constant.2.clone.table_ref, ...), custom_call_target="tpu_custom_call", output_to_operand_aliasing={{1}: (12, {}), {2}: (13, {})} | custom-call | tf_op jit(solution)/shard_map/attention_layer/pallas_call | solution.py:157
  92.1 51.8 %moe_layer.3 = bf16[64,2048]{1,0:T(8,128)(2,1)} custom-call(bf16[64,2048]{1,0:T(8,128)(2,1)} %get-tuple-element.12.x_ref, s32[2,8,64]{2,1,0:T(8,128)} %bitcast.5, f32[2,2048]{1,0:T(2,128)} %gain_ref.3, bf16[64,2048]{1,0:T(8,128)(2,1)} %bitcast.3, bf16[8,2048,1024]{2,1,0:T(8,128)(2,1)} %wg.3, bf16[8,2048,1024]{2,1,0:T(8,128)(2,1)} %wu.3, ...), custom_call_target="tpu_custom_call" | custom-call | tf_op jit(solution)/shard_map/moe_layer/pallas_call | solution.py:434
  143.9 1.7 %copy.26 = bf16[64,2048]{1,0:T(8,128)(2,1)} copy(bf16[64,2048]{1,0:T(8,128)(2,1)} %moe_layer.3) | data formatting | bytes 524288

commit v2 on v1

--- a/solution.py
+++ b/solution.py
@@ -20,7 +20,9 @@
 FORWARD_LAG = 5
 COLS = 512
 CACHE_BLOCKS = 4
-ATTEND_UNROLL = 8
+SCORE_UNROLL = 8
+MIX_UNROLL = 8
+WO_AFTER = 1
 
 
 def rms_norm(values, gain_vec):
@@ -39,7 +41,7 @@
 
 def attention_kernel(layer, aliased, pos_ref, x_ref, table_ref, attn_gain, q_gain, k_gain, wq, wk, wv, wo, k_in, v_in, *rest):
     rest = rest[2:] if aliased else rest
-    x_out, k_out, v_out, wbuf, kbuf, vbuf, proj, q_rows, k_rows, v_rows, mixed_rows, mixed, cos_ref, sin_ref, w_sem, in_sem, out_sem = rest
+    x_hbm, k_out, v_out, x_out, x_sem, wbuf, kbuf, vbuf, proj, q_rows, k_rows, v_rows, mixed_rows, mixed, probs, cos_ref, sin_ref, w_sem, in_sem, out_sem = rest
     seqs, model = x_ref.shape
     cache_len, heads, head_dim = kbuf.shape[1:]
     cols = wbuf.shape[2]
@@ -47,6 +49,9 @@
     block = seqs // CACHE_BLOCKS
 
     def weight_copy(index):
+        if not isinstance(index, int):
+            at = pl.ds(pl.multiple_of((index - 2 * chunks) * cols, cols), cols)
+            return pltpu.make_async_copy(wv.at[layer, :, at], wbuf.at[index], w_sem.at[index])
         weights = (wq, wk, wv, wo)[index // chunks]
         return pltpu.make_async_copy(weights.at[layer, :, pl.ds((index % chunks) * cols, cols)], wbuf.at[index], w_sem.at[index])
 
@@ -60,13 +65,15 @@
         part = pl.ds(i * block, block)
         return pltpu.make_async_copy(source.at[part], target.at[layer, part], out_sem.at[kind, i])
 
-    for index in range(3 * chunks):
+    for index in range(2 * chunks):
         weight_copy(index).start()
-    for i in range(CACHE_BLOCKS):
-        for kind in range(2):
-            cache_in(kind, i).start()
-    for index in range(3 * chunks, 4 * chunks):
-        weight_copy(index).start()
+    later = [[cache_in(0, i) for i in range(CACHE_BLOCKS)], [weight_copy(index) for index in range(2 * chunks, 3 * chunks)], [cache_in(1, i) for i in range(CACHE_BLOCKS)]]
+
+    def issue_next():
+        if later:
+            for copy in later.pop(0):
+                copy.start()
+
 
     for b in range(seqs):
         position = pos_ref[b]
@@ -79,6 +86,7 @@
             if c % 2 == 0:
                 weight_copy(kind * chunks + c).wait()
                 weight_copy(kind * chunks + c + 1).wait()
+                issue_next()
             proj[kind, :, c * cols:(c + 1) * cols] = jnp.dot(normed, wbuf[kind * chunks + c], preferred_element_type=jnp.float32)
 
     def rotate(kind, gain, target):
@@ -95,37 +103,58 @@
     rotate(0, q_gain, q_rows)
     project(1)
     rotate(1, k_gain, k_rows)
-    project(2)
+
+    scale = head_dim ** -0.5
+    row_iota = lax.broadcasted_iota(jnp.int32, (cache_len, heads, 1), 0)
+
+    def rows_of(b):
+        return pl.ds(pl.multiple_of(b * heads, heads), heads)
+
+    def score(b):
+        position = pos_ref[b]
+        kbuf[b, position] = k_rows[rows_of(b), :].astype(jnp.bfloat16)
+        scores = jnp.sum(kbuf[b].astype(jnp.float32) * q_rows[rows_of(b), :][None], axis=-1, keepdims=True) * scale
+        scores = jnp.where(row_iota <= position, scores, -1e30)
+        weights = jnp.exp(scores - jnp.max(scores, axis=0, keepdims=True))
+        prob = weights / jnp.sum(weights, axis=0, keepdims=True)
+        probs[b] = jnp.broadcast_to(prob, probs.shape[1:]).astype(jnp.bfloat16)
+
+    def mix(b):
+        vbuf[b, pos_ref[b]] = v_rows[rows_of(b), :].astype(jnp.bfloat16)
+        mixed_rows[rows_of(b), :] = jnp.sum(probs[b].astype(jnp.float32) * vbuf[b].astype(jnp.float32), axis=0)
+
+    def value_chunk(c):
+        weight_copy(2 * chunks + c).wait()
+        at = pl.ds(pl.multiple_of(c * cols, cols), cols)
+        proj[2, :, at] = jnp.dot(normed, wbuf[2 * chunks + c], preferred_element_type=jnp.float32)
+
+    trips = CACHE_BLOCKS * (block // SCORE_UNROLL)
+
+    def sweep(kind, step, unroll):
+        for i in range(CACHE_BLOCKS):
+            cache_in(kind, i).wait()
+            if kind == 0 and i == WO_AFTER:
+                for index in range(3 * chunks, 4 * chunks):
+                    weight_copy(index).start()
+
+            def body(outer, carry):
+                first = trips - chunks
+                trip = i * (block // unroll)
+                if kind == 0 and trip >= first:
+                    value_chunk(trip - first + outer)
+                for u in range(unroll):
+                    step(i * block + outer * unroll + u)
+                return carry
+
+            lax.fori_loop(0, block // unroll, body, 0)
+            if kind == 1:
+                cache_out(0, i).start()
+                cache_out(1, i).start()
+
+    sweep(0, score, SCORE_UNROLL)
     for h in range(heads):
         v_rows[pl.ds(h, seqs, stride=heads), :] = proj[2, :, h * head_dim:(h + 1) * head_dim]
-
-    scale = head_dim ** -0.5
-    row_iota = lax.broadcasted_iota(jnp.int32, (cache_len, heads, 1), 0)
-
-    def attend(b):
-        position = pos_ref[b]
-        at = pl.ds(pl.multiple_of(b * heads, heads), heads)
-        kbuf[b, position] = k_rows[at, :].astype(jnp.bfloat16)
-        vbuf[b, position] = v_rows[at, :].astype(jnp.bfloat16)
-        scores = jnp.sum(kbuf[b].astype(jnp.float32) * q_rows[at, :][None], axis=-1, keepdims=True) * scale
-        scores = jnp.where(row_iota <= position, scores, -1e30)
-        weights = jnp.exp(scores - jnp.max(scores, axis=0, keepdims=True))
-        prob = (weights / jnp.sum(weights, axis=0, keepdims=True)).astype(jnp.bfloat16).astype(jnp.float32)
-        mixed_rows[at, :] = jnp.sum(prob * vbuf[b].astype(jnp.float32), axis=0)
-
-    for i in range(CACHE_BLOCKS):
-        for kind in range(2):
-            cache_in(kind, i).wait()
-
-        def body(step, carry):
-            for u in range(ATTEND_UNROLL):
-                attend(i * block + step * ATTEND_UNROLL + u)
-            return carry
-
-        lax.fori_loop(0, block // ATTEND_UNROLL, body, 0)
-        for kind in range(2):
-            cache_out(kind, i).start()
-
+    sweep(1, mix, MIX_UNROLL)
     for h in range(heads):
         mixed[:, h * head_dim:(h + 1) * head_dim] = mixed_rows[pl.ds(h, seqs, stride=heads), :].astype(jnp.bfloat16)
     for c in range(chunks):
@@ -134,9 +163,12 @@
         at = slice(c * cols, (c + 1) * cols)
         added = jnp.dot(mixed[...], wbuf[3 * chunks + c], preferred_element_type=jnp.float32)
         x_out[:, at] = (x_ref[:, at].astype(jnp.float32) + added).astype(jnp.bfloat16)
+    result = pltpu.make_async_copy(x_out, x_hbm, x_sem)
+    result.start()
     for i in range(CACHE_BLOCKS):
         for kind in range(2):
             cache_out(kind, i).wait()
+    result.wait()
 
 
 def attention_local(layer, hidden, positions, table, attn_gain, q_gain, k_gain, w_query, w_key, w_value, w_out, k_cache, v_cache, k_new, v_new):
@@ -158,9 +190,11 @@
         functools.partial(attention_kernel, layer, bool(aliases)),
         out_shape=(jax.ShapeDtypeStruct(hidden.shape, hidden.dtype), jax.ShapeDtypeStruct(k_cache.shape, k_cache.dtype), jax.ShapeDtypeStruct(v_cache.shape, v_cache.dtype)),
         in_specs=specs,
-        out_specs=(vmem, hbm, hbm),
+        out_specs=(hbm, hbm, hbm),
         input_output_aliases=aliases,
         scratch_shapes=[
+            pltpu.VMEM(hidden.shape, hidden.dtype),
+            pltpu.SemaphoreType.DMA,
             pltpu.VMEM((4 * chunks, model, COLS), jnp.bfloat16),
             pltpu.VMEM(cache_shape, jnp.bfloat16),
             pltpu.VMEM(cache_shape, jnp.bfloat16),
@@ -170,6 +204,7 @@
             pltpu.VMEM((seqs * heads, head_dim), jnp.float32),
             pltpu.VMEM((seqs * heads, head_dim), jnp.float32),
             pltpu.VMEM((seqs, model), jnp.bfloat16),
+            pltpu.VMEM(cache_shape, jnp.bfloat16),
             pltpu.VMEM((seqs, head_dim), jnp.float32),
             pltpu.VMEM((seqs, head_dim), jnp.float32),
             pltpu.SemaphoreType.DMA((4 * chunks,)),
@@ -181,7 +216,7 @@
     )(*operands)
 
 
-def moe_kernel(groups, layer, x_ref, routes_ref, gain_ref, wr_ref, wg, wu, wd, out_ref, ring, rows, xg, act, ys, smat, meta, meta_in, part, dbuf, tbuf, f1, f2, ring_sem, down_sem, ag_send, ag_recv, meta_send, meta_recv, rs_send, rs_recv):
+def moe_kernel(groups, layer, x_ref, routes_ref, gain_ref, wr_ref, wg, wu, wd, out_hbm, out_ref, out_sem, ring, rows, xg, act, ys, smat, meta, meta_in, part, dbuf, tbuf, f1, f2, ring_sem, down_sem, ag_send, ag_recv, meta_send, meta_recv, rs_send, rs_recv):
     seqs, model = x_ref.shape
     local_experts = wg.shape[0]
     experts = wr_ref.shape[0]
@@ -408,18 +443,26 @@
         if k >= FORWARD_LAG:
             forward(k - FORWARD_LAG)
     pair_sum(RS_CHUNKS - 1)
-    for k in range(RS_CHUNKS - FORWARD_LAG, RS_CHUNKS):
-        forward(k)
-    for k in range(RS_CHUNKS):
-        finish(k)
     for group in copies:
         for copy in group:
             copy.wait_send()
     for copy in meta_copies:
         copy.wait_send()
+    for k in range(RS_CHUNKS - FORWARD_LAG):
+        for make in (pair_copy, far_copy, short_copy):
+            make(k).wait_send()
+    for k in range(RS_CHUNKS - FORWARD_LAG, RS_CHUNKS):
+        forward(k)
     for k in range(RS_CHUNKS):
-        for make in (pair_copy, far_copy, short_copy, long_copy):
-            make(k).wait_send()
+        finish(k)
+    result = pltpu.make_async_copy(out_ref, out_hbm, out_sem)
+    result.start()
+    for k in range(RS_CHUNKS):
+        if k >= RS_CHUNKS - FORWARD_LAG:
+            for make in (pair_copy, far_copy, short_copy):
+                make(k).wait_send()
+        long_copy(k).wait_send()
+    result.wait()
 
 
 def moe_local(hidden, routes, mlp_gain, w_router, w_gate, w_up, w_down, groups, layer):
@@ -435,8 +478,10 @@
         functools.partial(moe_kernel, groups, layer),
         out_shape=jax.ShapeDtypeStruct((seqs, model), jnp.bfloat16),
         in_specs=[vmem, vmem, vmem, vmem, hbm, hbm, hbm],
-        out_specs=vmem,
+        out_specs=hbm,
         scratch_shapes=[
+            pltpu.VMEM((seqs, model), jnp.bfloat16),
+            pltpu.SemaphoreType.DMA,
             pltpu.VMEM((RING, UNIT, ffn), jnp.bfloat16),
             pltpu.VMEM((groups, seqs, model), jnp.bfloat16),
             pltpu.VMEM((local_experts, groups * slots, model), jnp.bfloat16),

time: 146 us -> 142 us (0.973)
  Pallas kernels: 143 us -> 139 us
    pallas_call x2, Pallas kernels: 38.1 us -> 34.3 us  [attention_local(): pl.pallas_call(functools.partial(attention_kernel, layer, bool(aliases)),...]
where the time goes in v2:
time: 142 us; the launch traced here: 141 us
  Pallas kernels  139 us (98%)
  local copies, waits for them, and re-layouts  1.67 us (1%)
    pallas_call x2, Pallas kernels, moe_local(): pl.pallas_call(functools.partial(moe_kernel, groups, layer), out_shape=ja...  105 us
    pallas_call x2, Pallas kernels, attention_local(): pl.pallas_call(functools.partial(attention_kernel, layer, bool(aliases)),...  34.3 us

profile of v2, /device:TPU:113, one launch (start us, length us, event | category | flops | bytes accessed | tf_op | source)
XLA Modules:
  0.0 141.4 jit_solution(10875135211050075509)
XLA Ops:
  0.6 17.2 %attention_layer.2 = (bf16[64,2048]{1,0:T(8,128)(2,1)}, bf16[2,64,16,16,128]{4,3,2,1,0:T(8,128)(2,1)}, bf16[2,64,16,16,128]{4,3,2,1,0:T(8,128)(2,1)}) custom-call(s32[64]{0:T(128)} %pos_ref.3, bf16[64,2048]{1,0:T(8,128)(2,1)} %x_ref.1, f32[32,128]{1,0:T(8,128)} %constant.2.clone.table_ref, f32[2,2048]{1,0:T(2,128)} %attn_gain.3, f32[2,2048]{1,0:T(2,128)} %q_gain.3, ...), custom_call_target="tpu_custom_call" | custom-call | tf_op jit(solution)/shard_map/attention_layer/pallas_call | solution.py:189
  17.8 53.3 %moe_layer.2.x_ref = bf16[64,2048]{1,0:T(8,128)(2,1)} custom-call(bf16[64,2048]{1,0:T(8,128)(2,1)} %get-tuple-element.9.x_ref, s32[2,8,64]{2,1,0:T(8,128)} %bitcast.4, f32[2,2048]{1,0:T(2,128)} %gain_ref.3, bf16[64,2048]{1,0:T(8,128)(2,1)} %bitcast.2, bf16[8,2048,1024]{2,1,0:T(8,128)(2,1)} %wg.3, bf16[8,2048,1024]{2,1,0:T(8,128)(2,1)} %wu.3, ...), custom_call_target="tpu_custom_call" | custom-call | tf_op jit(solution)/shard_map/moe_layer/pallas_call | solution.py:477
  71.2 17.1 %attention_layer.3 = (bf16[64,2048]{1,0:T(8,128)(2,1)}, bf16[2,64,16,16,128]{4,3,2,1,0:T(8,128)(2,1)}, bf16[2,64,16,16,128]{4,3,2,1,0:T(8,128)(2,1)}) custom-call(s32[64]{0:T(128)} %pos_ref.3, bf16[64,2048]{1,0:T(8,128)(2,1)} %moe_layer.2.x_ref, f32[32,128]{1,0:T(8,128)} %constant.2.clone.table_ref, ...), custom_call_target="tpu_custom_call", output_to_operand_aliasing={{1}: (12, {}), {2}: (13, {})} | custom-call | tf_op jit(solution)/shard_map/attention_layer/pallas_call | solution.py:189
  88.3 51.5 %moe_layer.3 = bf16[64,2048]{1,0:T(8,128)(2,1)} custom-call(bf16[64,2048]{1,0:T(8,128)(2,1)} %get-tuple-element.12.x_ref, s32[2,8,64]{2,1,0:T(8,128)} %bitcast.5, f32[2,2048]{1,0:T(2,128)} %gain_ref.3, bf16[64,2048]{1,0:T(8,128)(2,1)} %bitcast.3, bf16[8,2048,1024]{2,1,0:T(8,128)(2,1)} %wg.3, bf16[8,2048,1024]{2,1,0:T(8,128)(2,1)} %wu.3, ...), custom_call_target="tpu_custom_call" | custom-call | tf_op jit(solution)/shard_map/moe_layer/pallas_call | solution.py:477
  139.7 1.7 %copy.26 = bf16[64,2048]{1,0:T(8,128)(2,1)} copy(bf16[64,2048]{1,0:T(8,128)(2,1)} %moe_layer.3) | data formatting | bytes 524288

commit v3 on v2

--- a/solution.py
+++ b/solution.py
@@ -12,7 +12,7 @@
 ROPE_BASE = 10000.0
 CAP_FACTOR = 2
 MESH = pl.DeviceIdType.MESH
-AG_PARTS = 2
+AG_PARTS = 4
 RS_CHUNKS = 8
 UNIT = 1024
 RING = 20
@@ -89,7 +89,7 @@
                 issue_next()
             proj[kind, :, c * cols:(c + 1) * cols] = jnp.dot(normed, wbuf[kind * chunks + c], preferred_element_type=jnp.float32)
 
-    def rotate(kind, gain, target):
+    def rotate(kind, gain, target, factor):
         values = proj[kind]
         inv_rms = lax.rsqrt(jnp.mean(values * values, axis=-1, keepdims=True) + RMS_EPS)
         cosines, sines = cos_ref[...], sin_ref[...]
@@ -97,14 +97,13 @@
             at = slice(h * head_dim, (h + 1) * head_dim)
             head = proj[kind, :, at] * inv_rms * gain[layer:layer + 1, at]
             turned = head * cosines + pltpu.roll(head, head_dim // 2, 1) * sines
-            target[pl.ds(h, seqs, stride=heads), :] = turned.astype(jnp.bfloat16).astype(jnp.float32)
+            target[pl.ds(h, seqs, stride=heads), :] = turned.astype(jnp.bfloat16).astype(jnp.float32) * factor
 
     project(0)
-    rotate(0, q_gain, q_rows)
+    rotate(0, q_gain, q_rows, head_dim ** -0.5)
     project(1)
-    rotate(1, k_gain, k_rows)
-
-    scale = head_dim ** -0.5
+    rotate(1, k_gain, k_rows, 1.0)
+
     row_iota = lax.broadcasted_iota(jnp.int32, (cache_len, heads, 1), 0)
 
     def rows_of(b):
@@ -113,10 +112,10 @@
     def score(b):
         position = pos_ref[b]
         kbuf[b, position] = k_rows[rows_of(b), :].astype(jnp.bfloat16)
-        scores = jnp.sum(kbuf[b].astype(jnp.float32) * q_rows[rows_of(b), :][None], axis=-1, keepdims=True) * scale
+        scores = jnp.sum(kbuf[b].astype(jnp.float32) * q_rows[rows_of(b), :][None], axis=-1, keepdims=True)
         scores = jnp.where(row_iota <= position, scores, -1e30)
         weights = jnp.exp(scores - jnp.max(scores, axis=0, keepdims=True))
-        prob = weights / jnp.sum(weights, axis=0, keepdims=True)
+        prob = weights * (1.0 / jnp.sum(weights, axis=0, keepdims=True))
         probs[b] = jnp.broadcast_to(prob, probs.shape[1:]).astype(jnp.bfloat16)
 
     def mix(b):
@@ -158,8 +157,9 @@
     for h in range(heads):
         mixed[:, h * head_dim:(h + 1) * head_dim] = mixed_rows[pl.ds(h, seqs, stride=heads), :].astype(jnp.bfloat16)
     for c in range(chunks):
-        weight_copy(3 * chunks + c).wait()
-    for c in range(chunks):
+        if c % 2 == 0:
+            weight_copy(3 * chunks + c).wait()
+            weight_copy(3 * chunks + c + 1).wait()
         at = slice(c * cols, (c + 1) * cols)
         added = jnp.dot(mixed[...], wbuf[3 * chunks + c], preferred_element_type=jnp.float32)
         x_out[:, at] = (x_ref[:, at].astype(jnp.float32) + added).astype(jnp.bfloat16)

time: 142 us -> 141 us (level)
  no operation moved by 1% of the time
where the time goes in v3:
time: 141 us
  Pallas kernels  138 us (98%)
  local copies, waits for them, and re-layouts  1.67 us (1%)
    pallas_call x2, Pallas kernels, moe_local(): pl.pallas_call(functools.partial(moe_kernel, groups, layer), out_shape=ja...  104 us
    pallas_call x2, Pallas kernels, attention_local(): pl.pallas_call(functools.partial(attention_kernel, layer, bool(aliases)),...  33.9 us

profile of v3, /device:TPU:113, one launch (start us, length us, event | category | flops | bytes accessed | tf_op | source)
XLA Modules:
  0.0 140.6 jit_solution(3318624356768399821)
XLA Ops:
  0.6 17.0 %attention_layer.2 = (bf16[64,2048]{1,0:T(8,128)(2,1)}, bf16[2,64,16,16,128]{4,3,2,1,0:T(8,128)(2,1)}, bf16[2,64,16,16,128]{4,3,2,1,0:T(8,128)(2,1)}) custom-call(s32[64]{0:T(128)} %pos_ref.3, bf16[64,2048]{1,0:T(8,128)(2,1)} %x_ref.1, f32[32,128]{1,0:T(8,128)} %constant.2.clone.table_ref, f32[2,2048]{1,0:T(2,128)} %attn_gain.3, f32[2,2048]{1,0:T(2,128)} %q_gain.3, ...), custom_call_target="tpu_custom_call" | custom-call | tf_op jit(solution)/shard_map/attention_layer/pallas_call | solution.py:189
  17.6 52.8 %moe_layer.2.x_ref = bf16[64,2048]{1,0:T(8,128)(2,1)} custom-call(bf16[64,2048]{1,0:T(8,128)(2,1)} %get-tuple-element.9.x_ref, s32[2,8,64]{2,1,0:T(8,128)} %bitcast.4, f32[2,2048]{1,0:T(2,128)} %gain_ref.3, bf16[64,2048]{1,0:T(8,128)(2,1)} %bitcast.2, bf16[8,2048,1024]{2,1,0:T(8,128)(2,1)} %wg.3, bf16[8,2048,1024]{2,1,0:T(8,128)(2,1)} %wu.3, ...), custom_call_target="tpu_custom_call" | custom-call | tf_op jit(solution)/shard_map/moe_layer/pallas_call | solution.py:477
  70.4 16.9 %attention_layer.3 = (bf16[64,2048]{1,0:T(8,128)(2,1)}, bf16[2,64,16,16,128]{4,3,2,1,0:T(8,128)(2,1)}, bf16[2,64,16,16,128]{4,3,2,1,0:T(8,128)(2,1)}) custom-call(s32[64]{0:T(128)} %pos_ref.3, bf16[64,2048]{1,0:T(8,128)(2,1)} %moe_layer.2.x_ref, f32[32,128]{1,0:T(8,128)} %constant.2.clone.table_ref, ...), custom_call_target="tpu_custom_call", output_to_operand_aliasing={{1}: (12, {}), {2}: (13, {})} | custom-call | tf_op jit(solution)/shard_map/attention_layer/pallas_call | solution.py:189
  87.4 51.5 %moe_layer.3 = bf16[64,2048]{1,0:T(8,128)(2,1)} custom-call(bf16[64,2048]{1,0:T(8,128)(2,1)} %get-tuple-element.12.x_ref, s32[2,8,64]{2,1,0:T(8,128)} %bitcast.5, f32[2,2048]{1,0:T(2,128)} %gain_ref.3, bf16[64,2048]{1,0:T(8,128)(2,1)} %bitcast.3, bf16[8,2048,1024]{2,1,0:T(8,128)(2,1)} %wg.3, bf16[8,2048,1024]{2,1,0:T(8,128)(2,1)} %wu.3, ...), custom_call_target="tpu_custom_call" | custom-call | tf_op jit(solution)/shard_map/moe_layer/pallas_call | solution.py:477
  138.9 1.7 %copy.26 = bf16[64,2048]{1,0:T(8,128)(2,1)} copy(bf16[64,2048]{1,0:T(8,128)(2,1)} %moe_layer.3) | data formatting | bytes 524288

commit v4 on v3

--- a/solution.py
+++ b/solution.py
@@ -17,7 +17,7 @@
 UNIT = 1024
 RING = 20
 LANES = 128
-FORWARD_LAG = 5
+FORWARD_LAG = 6
 COLS = 512
 CACHE_BLOCKS = 4
 SCORE_UNROLL = 8
@@ -75,10 +75,13 @@
                 copy.start()
 
 
-    for b in range(seqs):
+    def table_row(b, carry):
         position = pos_ref[b]
-        cos_ref[b:b + 1, :] = table_ref[pl.ds(position, 1), :]
-        sin_ref[b:b + 1, :] = table_ref[pl.ds(position + cache_len, 1), :]
+        cos_ref[pl.ds(b, 1), :] = table_ref[pl.ds(position, 1), :]
+        sin_ref[pl.ds(b, 1), :] = table_ref[pl.ds(position + cache_len, 1), :]
+        return carry
+
+    lax.fori_loop(0, seqs, table_row, 0)
     normed = rms_norm(x_ref[...], attn_gain[layer:layer + 1, :]).astype(jnp.bfloat16)
 
     def project(kind):

time: 141 us -> 141 us (level)
  no operation moved by 1% of the time
where the time goes in v4:
time: 141 us; the launch traced here: 140 us
  Pallas kernels  138 us (98%)
  local copies, waits for them, and re-layouts  1.67 us (1%)
    pallas_call x2, Pallas kernels, moe_local(): pl.pallas_call(functools.partial(moe_kernel, groups, layer), out_shape=ja...  104 us
    pallas_call x2, Pallas kernels, attention_local(): pl.pallas_call(functools.partial(attention_kernel, layer, bool(aliases)),...  33.9 us

profile of v4, /device:TPU:113, one launch (start us, length us, event | category | flops | bytes accessed | tf_op | source)
XLA Modules:
  0.0 140.4 jit_solution(3381199960806315497)
XLA Ops:
  0.6 16.9 %attention_layer.2 = (bf16[64,2048]{1,0:T(8,128)(2,1)}, bf16[2,64,16,16,128]{4,3,2,1,0:T(8,128)(2,1)}, bf16[2,64,16,16,128]{4,3,2,1,0:T(8,128)(2,1)}) custom-call(s32[64]{0:T(128)} %pos_ref.3, bf16[64,2048]{1,0:T(8,128)(2,1)} %x_ref.1, f32[32,128]{1,0:T(8,128)} %constant.2.clone.table_ref, f32[2,2048]{1,0:T(2,128)} %attn_gain.3, f32[2,2048]{1,0:T(2,128)} %q_gain.3, ...), custom_call_target="tpu_custom_call" | custom-call | tf_op jit(solution)/shard_map/attention_layer/pallas_call | solution.py:192
  17.6 52.8 %moe_layer.2.x_ref = bf16[64,2048]{1,0:T(8,128)(2,1)} custom-call(bf16[64,2048]{1,0:T(8,128)(2,1)} %get-tuple-element.9.x_ref, s32[2,8,64]{2,1,0:T(8,128)} %bitcast.4, f32[2,2048]{1,0:T(2,128)} %gain_ref.3, bf16[64,2048]{1,0:T(8,128)(2,1)} %bitcast.2, bf16[8,2048,1024]{2,1,0:T(8,128)(2,1)} %wg.3, bf16[8,2048,1024]{2,1,0:T(8,128)(2,1)} %wu.3, ...), custom_call_target="tpu_custom_call" | custom-call | tf_op jit(solution)/shard_map/moe_layer/pallas_call | solution.py:480
  70.4 16.9 %attention_layer.3 = (bf16[64,2048]{1,0:T(8,128)(2,1)}, bf16[2,64,16,16,128]{4,3,2,1,0:T(8,128)(2,1)}, bf16[2,64,16,16,128]{4,3,2,1,0:T(8,128)(2,1)}) custom-call(s32[64]{0:T(128)} %pos_ref.3, bf16[64,2048]{1,0:T(8,128)(2,1)} %moe_layer.2.x_ref, f32[32,128]{1,0:T(8,128)} %constant.2.clone.table_ref, ...), custom_call_target="tpu_custom_call", output_to_operand_aliasing={{1}: (12, {}), {2}: (13, {})} | custom-call | tf_op jit(solution)/shard_map/attention_layer/pallas_call | solution.py:192
  87.3 51.4 %moe_layer.3 = bf16[64,2048]{1,0:T(8,128)(2,1)} custom-call(bf16[64,2048]{1,0:T(8,128)(2,1)} %get-tuple-element.12.x_ref, s32[2,8,64]{2,1,0:T(8,128)} %bitcast.5, f32[2,2048]{1,0:T(2,128)} %gain_ref.3, bf16[64,2048]{1,0:T(8,128)(2,1)} %bitcast.3, bf16[8,2048,1024]{2,1,0:T(8,128)(2,1)} %wg.3, bf16[8,2048,1024]{2,1,0:T(8,128)(2,1)} %wu.3, ...), custom_call_target="tpu_custom_call" | custom-call | tf_op jit(solution)/shard_map/moe_layer/pallas_call | solution.py:480
  138.8 1.7 %copy.26 = bf16[64,2048]{1,0:T(8,128)(2,1)} copy(bf16[64,2048]{1,0:T(8,128)(2,1)} %moe_layer.3) | data formatting | bytes 524288
